TPU v7x, 256 devices: a whole 4x4x8 slice. The times are simulated.
256 devices in a mesh: paths: 8 (over x, core), cpty: 32 (over z, y).
Axes of the slice: x: 4, y: 4, z: 8, core: 2. Of those that a mesh axis runs over, the one named last changes fastest.
Arguments:
- factors: bfloat16 [64, 12288], P(None, 'paths'), may hold values from -6 to 6
- loadings: bfloat16 [64, 65536], P(None, 'cpty'), may hold values from -2 to 2
- notional: bfloat16 [65536], P('cpty'), may hold values from 0.25 to 0.796875
- strike: bfloat16 [65536], P('cpty'), may hold values from 2 to 8
- curvature: bfloat16 [65536], P('cpty'), may hold values from 1 to 3
- trade_cpty: int32 [65536], P('cpty'), may hold values from 0 to 4095, as said below
Outputs:
- exposure: bfloat16 [12288, 4096], P('paths', 'cpty')
- moment: float32 [4096, 4096], P('paths', 'cpty')
Inputs may be any that keep to these rules, and one draw needn't show every extreme that they name: `trade_cpty`: of the trades in the book of one index of cpty, at most 128 belong to the counterparties numbered k * 128 to (k + 1) * 128 - 1 for any k; in every draw some such k receives exactly 128 from every book.
All inputs are finite; a program needn't handle non-finite values.
Results may differ from a plain program's by a relative error of at most 0.0064.
Values may be sent and summed in bfloat16 or wider, within the bound.
A program may use at most 128 MiB of HBM per device.

v0:
```python
import jax
import jax.numpy as jnp
from jax import lax
from jax.sharding import PartitionSpec as P

CP_DEV = 128


def in_blocks(x, dim, length):
    before, after = (x.shape[:dim], x.shape[dim + 1 :])
    return jnp.moveaxis(x.reshape(*before, length, -1, *after), dim, 0)


def summed_on_arrival(x, axis, dim):
    parts = in_blocks(x, dim, lax.axis_size(axis))
    arrived = lax.all_to_all(parts, axis, split_axis=0, concat_axis=0, tiled=True)
    return arrived.astype(jnp.float32).sum(axis=0)


def price_trades(drivers, loading_cols, trade_terms):
    linear = jnp.dot(drivers, loading_cols, preferred_element_type=jnp.float32)
    terms_wide = trade_terms.astype(jnp.float32)
    value = terms_wide[0] * (linear + terms_wide[2] * jnp.tanh(linear - terms_wide[1]))
    return value.astype(jnp.bfloat16)


def on_device(factors, loadings, notional, strike, curvature, trade_cpty):
    groups = lax.axis_size("cpty")
    own_index = lax.axis_index("cpty")
    trades = loadings.shape[1]
    slot_size = 2 * trades // groups
    owners = trade_cpty // CP_DEV
    marked = (owners[:, None] == jnp.arange(groups, dtype=jnp.int32)[None, :]).astype(jnp.int32)
    ranking = jnp.sum((jnp.cumsum(marked, axis=0) - marked) * marked, axis=1)
    target = owners * slot_size + ranking
    chosen = (
        jnp.zeros((groups * slot_size,), jnp.int32)
        .at[target]
        .set(jnp.arange(trades, dtype=jnp.int32))
    )
    filled = jnp.zeros((groups * slot_size,), jnp.bool_).at[target].set(True)
    labels = jnp.where(filled, trade_cpty[chosen], -1)[None, :]
    drivers = jnp.transpose(factors)
    trade_terms = jnp.stack([notional, strike, curvature])
    described = jnp.concatenate([loadings, trade_terms], axis=0)
    packed = jnp.where(
        filled[None, :], jnp.take(described, chosen, axis=1), jnp.zeros((), jnp.bfloat16)
    )
    received, arrived_ids = (
        lax.all_to_all(packed, "cpty", split_axis=1, concat_axis=1, tiled=True),
        lax.all_to_all(labels, "cpty", split_axis=1, concat_axis=1, tiled=True),
    )
    factor_count = loadings.shape[0]
    arrived = price_trades(drivers, received[:factor_count], received[factor_count:])
    local_ids = arrived_ids[0] - own_index * CP_DEV
    onehot = (local_ids[:, None] == jnp.arange(CP_DEV, dtype=jnp.int32)[None, :]).astype(
        jnp.bfloat16
    )
    netted = jnp.dot(arrived, onehot, preferred_element_type=jnp.float32)
    exposure = jnp.maximum(netted, 0.0).astype(jnp.bfloat16)
    everyone = lax.all_gather(exposure, "cpty", axis=1, tiled=True)
    path_total = exposure.shape[0] * lax.axis_size("paths")
    moment = (
        summed_on_arrival(
            jnp.einsum("pa,pb->ab", everyone, exposure, preferred_element_type=jnp.float32).astype(
                jnp.bfloat16
            ),
            "paths",
            0,
        )
        / path_total
    )
    return (exposure, moment)


def solution(mesh):
    in_specs = (P(None, "paths"), P(None, "cpty"), P("cpty"), P("cpty"), P("cpty"), P("cpty"))
    out_specs = (P("paths", "cpty"), P("paths", "cpty"))
    return jax.shard_map(
        on_device, mesh=mesh, in_specs=in_specs, out_specs=out_specs, check_vma=False
    )
```

profile of v0, /device:TPU:1, one launch (start us, length us, event | category | flops | bytes accessed | tf_op | source)
XLA Modules:
  0.0 287.2 jit_solution(17059434159926769436)
XLA Ops:
  7.2 0.0 copy-start
  7.2 0.0 copy-start.1
  7.2 0.0 copy-start.2
  7.2 0.0 copy-start.3
  7.2 0.0 copy-start.4
  7.2 0.0 copy-start.5
  7.2 0.8 add_select_fusion
  8.0 9.1 %reduce-window.6 = s32[32,16,128]{2,1,0:T(8,128)S(1)} reduce-window(s32[32,16,128]{2,1,0:T(8,128)S(1)} %fusion.18, s32[]{:T(128)} %constant.24.clone.1), window={size=1x1x128 pad=0_0x0_0x127_0}, to_apply=%region_0.1 | reduce-window | flops 8323072 | bytes 524292 | tf_op jit(solution)/shard_map/reduce-window
  17.1 0.1 slice.40
  17.2 0.2 copy.33
  17.5 0.2 reduce-window.9
  17.7 0.1 broadcast_add_fusion
  17.8 0.1 fusion.17
  17.9 0.7 compare_select_fusion.1
  18.7 8.1 %scatter_custom_fusion.1 = s32[4096]{0:T(1024)S(1)} fusion(s32[2048]{0:T(1024)S(1)} %compare_select_fusion.1, s32[2048]{0:T(1024)S(1)} %iota.15, s32[]{:T(128)} %constant.24.clone.1), kind=kCustom, calls=%fused_computation.49 | custom fusion | bytes 16388 | tf_op jit(solution)/shard_map/scatter | solution.py:39
  26.7 0.0 copy-done.1
  26.7 23.0 %gather_fusion.1 = s32[4096]{0:T(1024)S(1)} fusion(s32[2048]{0:T(1024)S(1)} %copy-done.1, s32[4096]{0:T(1024)S(1)} %fusion.19), kind=kCustom, calls=%fused_computation.1 | custom fusion | bytes 49152 | tf_op jit(solution)/shard_map/gather | solution.py:42
  49.8 9.1 %scatter_custom_fusion = pred[4096]{0:T(1024)(128)(4,1)S(1)} fusion(s32[2048]{0:T(1024)S(1)} %compare_select_fusion.1, pred[2048]{0:T(1024)(128)(4,1)S(1)} %broadcast.49, pred[]{:T(512)} %constant.22.clone.1), kind=kCustom, calls=%fused_computation.53 | custom fusion | bytes 4097 | tf_op jit(solution)/shard_map/scatter | solution.py:41
  58.9 0.6 broadcast_select_fusion
  59.5 12.0 %all-to-all-start.1 = ((s32[1,32,128]{2,0,1:T(1,128)}), s32[1,32,128]{2,0,1:T(1,128)S(1)}, u32[]{:S(2)}, u32[]{:S(2)}) async-start(s32[1,32,128]{2,0,1:T(1,128)} %bitcast.12), calls=%async_computation.1 | async-start | bytes 32768 | tf_op jit(solution)/shard_map/all_to_all | solution.py:51
  71.6 0.0 copy-done.2
  71.6 0.3 copy.26
  71.9 0.0 copy-done.3
  71.9 0.3 stack.12
  72.2 0.0 copy-done.4
  72.3 0.3 stack.13
  72.6 0.0 copy-done.5
  72.6 0.3 stack.14
  72.9 0.7 pad_maximum_fusion
  73.7 12.1 %gather_fusion = bf16[4096,67]{1,0:T(8,128)(2,1)S(1)} fusion(bf16[67,2048]{0,1:T(8,128)(2,1)S(1)} %pad_maximum_fusion, s32[4096]{0:T(1024)S(1)} %fusion.19), kind=kCustom, calls=%fused_computation | custom fusion | bytes 1114112 | tf_op jit(solution)/shard_map/jit(_take)/gather | solution.py:47
  85.8 0.6 copy.30
  86.4 0.9 select_select_fusion
  87.3 0.0 all-to-all-done.1
  87.3 9.2 %all-to-all-start = ((bf16[67,32,128]{2,0,1:T(8,128)(2,1)}), bf16[67,32,128]{2,0,1:T(8,128)(2,1)S(1)}, u32[]{:S(2)}, u32[]{:S(2)}) async-start(bf16[67,32,128]{2,0,1:T(8,128)(2,1)} %select_select_fusion), calls=%async_computation | async-start | bytes 1179648 | tf_op jit(solution)/shard_map/all_to_all | solution.py:50
  96.6 0.0 all-gather.2.cloned.1.call-start
  96.6 0.9 iota_compare_fusion.7
  97.5 15.6 %all-to-all-done = bf16[67,32,128]{2,0,1:T(8,128)(2,1)S(1)} async-done(((bf16[67,32,128]{2,0,1:T(8,128)(2,1)}), bf16[67,32,128]{2,0,1:T(8,128)(2,1)S(1)}, u32[]{:S(2)}, u32[]{:S(2)}) %all-to-all-start) | async-done | bytes 548896 | tf_op jit(solution)/shard_map/all_to_all | solution.py:50
  113.2 0.0 copy-done
  113.2 14.0 %fusion.9 = bf16[1536,128]{1,0:T(8,128)(2,1)} fusion(bf16[64,1536]{1,0:T(8,128)(2,1)S(1)} %copy-done, f32[4096]{0:T(1024)S(1)} %get-tuple-element.3, f32[4096]{0:T(1024)S(1)} %get-tuple-element.4, f32[4096]{0:T(1024)S(1)} %get-tuple-element.2, bf16[67,32,128]{2,0,1:T(8,128)(2,1)S(1)} %all-to-all-done, pred[4096,128]{1,0:T(32,128)(4,1)S(1)} %iota_compare_fusion.7), kind=kOutput, calls=%fused_computation.16 | convolution fusion | flops 2447769600 | bytes 1687552 | tf_op jit(solution)/shard_map/dot_general | solution.py:59
  127.2 0.0 all-gather.2.cloned.1.call-update
  127.2 121.3 %all-gather.2.cloned.1.call-done = bf16[1536,4096]{1,0:T(8,128)(2,1)} async-done(((bf16[1536,128]{1,0:T(8,128)(2,1)}), bf16[1536,4096]{1,0:T(8,128)(2,1)}) %all-gather.2.cloned.1.call-update) | async-done | bytes 12582928 | tf_op jit(solution)/shard_map/all_gather | solution.py:61
  248.5 8.1 %convolution_convert_fusion = bf16[4096,128]{1,0:T(8,128)(2,1)S(1)} fusion(bf16[1536,4096]{1,0:T(8,128)(2,1)} %all-gather.2.cloned.1.call-done, bf16[1536,128]{1,0:T(8,128)(2,1)} %fusion.9), kind=kOutput, calls=%fused_computation.14 | convolution fusion | flops 1611137024 | bytes 14024704 | tf_op jit(solution)/shard_map/pa,pb->ab/dot_general | solution.py:65
  256.5 23.0 %all_to_all.20 = bf16[8,512,128]{2,1,0:T(8,128)(2,1)S(1)} all-to-all(bf16[8,512,128]{2,1,0:T(8,128)(2,1)S(1)} %bitcast.86), channel_id=1, replica_groups=mesh['paths'=8,'cpty'=32] {'paths'}, dimensions={0} | all-to-all | bytes 2097152 | tf_op jit(solution)/shard_map/all_to_all | solution.py:16
  279.5 0.1 convert_reduce_fusion
  279.6 0.7 broadcast_multiply_fusion
  (9 shorter events, 0.1 us)
Async XLA Ops:
  7.2 106.0 %copy-start = (bf16[64,1536]{1,0:T(8,128)(2,1)S(1)}, bf16[64,1536]{1,0:T(8,128)(2,1)}, u32[]{:S(2)}) copy-start(bf16[64,1536]{1,0:T(8,128)(2,1)} %param.6) | copy-start | bytes 589828
  7.2 19.6 %copy-start.1 = (s32[2048]{0:T(1024)S(1)}, s32[2048]{0:T(1024)}, u32[]{:S(2)}) copy-start(s32[2048]{0:T(1024)} %param.11) | copy-start | bytes 24580
  7.2 64.4 %copy-start.2 = (bf16[64,2048]{1,0:T(8,128)(2,1)S(1)}, bf16[64,2048]{1,0:T(8,128)(2,1)}, u32[]{:S(2)}) copy-start(bf16[64,2048]{1,0:T(8,128)(2,1)} %param.7) | copy-start | bytes 786436
  7.2 64.7 %copy-start.3 = (bf16[2048]{0:T(1024)(128)(2,1)S(1)}, bf16[2048]{0:T(1024)(128)(2,1)}, u32[]{:S(2)}) copy-start(bf16[2048]{0:T(1024)(128)(2,1)} %param.8) | copy-start | bytes 12292
  7.2 65.0 %copy-start.4 = (bf16[2048]{0:T(1024)(128)(2,1)S(1)}, bf16[2048]{0:T(1024)(128)(2,1)}, u32[]{:S(2)}) copy-start(bf16[2048]{0:T(1024)(128)(2,1)} %param.9) | copy-start | bytes 12292
  7.2 65.4 %copy-start.5 = (bf16[2048]{0:T(1024)(128)(2,1)S(1)}, bf16[2048]{0:T(1024)(128)(2,1)}, u32[]{:S(2)}) copy-start(bf16[2048]{0:T(1024)(128)(2,1)} %param.10) | copy-start | bytes 12292
  59.5 27.8 %all-to-all-start.1 = ((s32[1,32,128]{2,0,1:T(1,128)}), s32[1,32,128]{2,0,1:T(1,128)S(1)}, u32[]{:S(2)}, u32[]{:S(2)}) async-start(s32[1,32,128]{2,0,1:T(1,128)} %bitcast.12), calls=%async_computation.1 | async-start | bytes 32768 | tf_op jit(solution)/shard_map/all_to_all | solution.py:51
  87.3 25.8 %all-to-all-start = ((bf16[67,32,128]{2,0,1:T(8,128)(2,1)}), bf16[67,32,128]{2,0,1:T(8,128)(2,1)S(1)}, u32[]{:S(2)}, u32[]{:S(2)}) async-start(bf16[67,32,128]{2,0,1:T(8,128)(2,1)} %select_select_fusion), calls=%async_computation | async-start | bytes 1179648 | tf_op jit(solution)/shard_map/all_to_all | solution.py:50
  96.6 151.9 %all-gather.2.cloned.1.call-start = ((), (), s32[]{:S(2)}) async-start(), calls=%async_computation.3 | async-start | bytes 12976128 | tf_op jit(solution)/shard_map/all_gather | solution.py:61
Sparse Core Ops, SparseCore 0:
  127.3 121.1 all-gather.1
where the time goes:
time: 288 us; the launch traced here: 287 us
  waiting for transfers between devices  137 us (48%)
  local copies, waits for them, and re-layouts  54.7 us (19%)
  blocking collectives  23 us (8%)
  matrix products  22.1 us (8%)
  starting transfers between devices  21.3 us (7%)
  other arithmetic  15 us (5%)
  between operations  14.3 us (5%)
    all_gather x1, waiting for transfers between devices, on_device(): everyone = lax.all_gather(exposure, 'cpty', axis=1, tiled=True)  121 us
    gather x1, local copies, waits for them, and re-layouts, on_device(): labels = jnp.where(filled, trade_cpty[chosen], -1)[None, :]  23 us
    all_to_all x1, blocking collectives, summed_on_arrival(): lax.all_to_all(parts, axis, split_axis=0, concat_axis=0, tiled=True)  23 us
    all_to_all x1, waiting for transfers between devices, on_device(): lax.all_to_all(packed, 'cpty', split_axis=1, concat_axis=1, tiled=True)  15.6 us
    dot_general x1, matrix products, on_device(): netted = jnp.dot(arrived, onehot, preferred_element_type=jnp.float32)  14 us
    gather x2, local copies, waits for them, and re-layouts, on_device(): jnp.take(described, chosen, axis=1)  12.8 us
    all_to_all x1, starting transfers between devices, on_device(): lax.all_to_all(labels, 'cpty', split_axis=1, concat_axis=1, tiled=True)  12 us
    another operation x3, other arithmetic  9.41 us
  transfers between devices with their start and end apart: 3, of which 2 were waited for; matrix products, arithmetic and copies ran while one was open for 6% of the time, Pallas kernels for 0%

commit v1 on v0

--- a/solution.py
+++ b/solution.py
@@ -58,7 +58,11 @@
     )
     netted = jnp.dot(arrived, onehot, preferred_element_type=jnp.float32)
     exposure = jnp.maximum(netted, 0.0).astype(jnp.bfloat16)
-    everyone = lax.all_gather(exposure, "cpty", axis=1, tiled=True)
+    size = lax.axis_size("cpty")
+    repeats = [size if d == 1 else 1 for d in range(exposure.ndim)]
+    everyone = lax.all_to_all(
+        jnp.tile(exposure, repeats), "cpty", split_axis=1, concat_axis=1, tiled=True
+    )
     path_total = exposure.shape[0] * lax.axis_size("paths")
     moment = (
         summed_on_arrival(

time: 288 us -> 454 us (1.58)
  blocking collectives: 23 us -> 302 us
  waiting for transfers between devices: 137 us -> 15.6 us
  local copies, waits for them, and re-layouts: 54.7 us -> 78.6 us
  between operations: 14.3 us -> 0.93 us
    all_to_all x0 -> x1, blocking collectives: none -> 279 us  [on_device(): lax.all_to_all(jnp.tile(exposure, repeats), 'cpty', split_axis=1, concat_...]
    all_gather x1 -> x0, waiting for transfers between devices: 121 us -> none  [on_device(): everyone = lax.all_gather(exposure, 'cpty', axis=1, tiled=True)]
    all_to_all x0 -> x1, local copies, waits for them, and re-layouts: none -> 16.6 us  [on_device(): lax.all_to_all(jnp.tile(exposure, repeats), 'cpty', split_axis=1, concat_...]
    another operation x1 -> x2, local copies, waits for them, and re-layouts: 0.24 us -> 7.54 us  [the longest x1 7.3 us: on_device(): jnp.tile(exposure, repeats)]
  transfers between devices with their start and end apart: 3 -> 2, of which waited for: 2 -> 1; matrix products, arithmetic and copies ran while one was open for 6% -> 4% of each run, Pallas kernels for 0% -> 0%
where the time goes in v1:
time: 454 us; the launch traced here: 453 us
  blocking collectives  302 us (67%)
  local copies, waits for them, and re-layouts  78.6 us (17%)
  starting transfers between devices  21.2 us (5%)
  matrix products  19.7 us (4%)
  waiting for transfers between devices  15.6 us (3%)
  other arithmetic  15 us (3%)
    all_to_all x1, blocking collectives, on_device(): lax.all_to_all(jnp.tile(exposure, repeats), 'cpty', split_axis=1, concat_...  279 us
    gather x1, local copies, waits for them, and re-layouts, on_device(): labels = jnp.where(filled, trade_cpty[chosen], -1)[None, :]  23 us
    all_to_all x1, blocking collectives, summed_on_arrival(): lax.all_to_all(parts, axis, split_axis=0, concat_axis=0, tiled=True)  22.6 us
    all_to_all x1, local copies, waits for them, and re-layouts, on_device(): lax.all_to_all(jnp.tile(exposure, repeats), 'cpty', split_axis=1, concat_...  16.6 us
    all_to_all x1, waiting for transfers between devices, on_device(): lax.all_to_all(packed, 'cpty', split_axis=1, concat_axis=1, tiled=True)  15.6 us
    dot_general x1, matrix products, on_device(): netted = jnp.dot(arrived, onehot, preferred_element_type=jnp.float32)  13.2 us
    gather x2, local copies, waits for them, and re-layouts, on_device(): jnp.take(described, chosen, axis=1)  12.7 us
    all_to_all x1, starting transfers between devices, on_device(): lax.all_to_all(labels, 'cpty', split_axis=1, concat_axis=1, tiled=True)  12 us
  transfers between devices with their start and end apart: 2, of which 1 were waited for; matrix products, arithmetic and copies ran while one was open for 4% of the time, Pallas kernels for 0%

profile of v1, /device:TPU:1, one launch (start us, length us, event | category | flops | bytes accessed | tf_op | source)
XLA Modules:
  0.0 452.8 jit_solution(9188662906149338010)
XLA Ops:
  0.6 0.0 copy-start
  0.6 0.0 copy-start.1
  0.7 0.0 copy-start.3
  0.7 0.0 copy-start.4
  0.7 0.0 copy-start.5
  0.7 0.0 copy-start.6
  0.7 0.8 add_select_fusion
  1.5 9.1 %reduce-window.6 = s32[32,16,128]{2,1,0:T(8,128)S(1)} reduce-window(s32[32,16,128]{2,1,0:T(8,128)S(1)} %fusion.18, s32[]{:T(128)} %constant.24.clone.1), window={size=1x1x128 pad=0_0x0_0x127_0}, to_apply=%region_0.1 | reduce-window | flops 8323072 | bytes 524292 | tf_op jit(solution)/shard_map/reduce-window
  10.6 0.1 slice.40
  10.7 0.2 copy.34
  11.0 0.2 reduce-window.9
  11.1 0.1 broadcast_add_fusion
  11.3 0.1 fusion.17
  11.4 0.7 compare_select_fusion.1
  12.1 8.1 %scatter_custom_fusion.1 = s32[4096]{0:T(1024)S(1)} fusion(s32[2048]{0:T(1024)S(1)} %compare_select_fusion.1, s32[2048]{0:T(1024)S(1)} %iota.15, s32[]{:T(128)} %constant.24.clone.1), kind=kCustom, calls=%fused_computation.49 | custom fusion | bytes 16388 | tf_op jit(solution)/shard_map/scatter | solution.py:39
  20.2 0.0 copy-done.1
  20.2 23.0 %gather_fusion.1 = s32[4096]{0:T(1024)S(1)} fusion(s32[2048]{0:T(1024)S(1)} %copy-done.1, s32[4096]{0:T(1024)S(1)} %fusion.19), kind=kCustom, calls=%fused_computation.1 | custom fusion | bytes 49152 | tf_op jit(solution)/shard_map/gather | solution.py:42
  43.3 9.1 %scatter_custom_fusion = pred[4096]{0:T(1024)(128)(4,1)S(1)} fusion(s32[2048]{0:T(1024)S(1)} %compare_select_fusion.1, pred[2048]{0:T(1024)(128)(4,1)S(1)} %broadcast.52, pred[]{:T(512)} %constant.22.clone.1), kind=kCustom, calls=%fused_computation.53 | custom fusion | bytes 4097 | tf_op jit(solution)/shard_map/scatter | solution.py:41
  52.4 0.6 broadcast_select_fusion
  53.0 12.0 %all-to-all-start.1 = ((s32[1,32,128]{2,0,1:T(1,128)}), s32[1,32,128]{2,0,1:T(1,128)S(1)}, u32[]{:S(2)}, u32[]{:S(2)}) async-start(s32[1,32,128]{2,0,1:T(1,128)} %bitcast.12), calls=%async_computation.1 | async-start | bytes 32768 | tf_op jit(solution)/shard_map/all_to_all | solution.py:51
  65.1 0.0 copy-done.3
  65.1 0.3 copy.26
  65.3 0.0 copy-done.4
  65.4 0.3 stack.12
  65.7 0.0 copy-done.5
  65.7 0.3 stack.13
  66.0 0.0 copy-done.6
  66.1 0.3 stack.14
  66.4 0.7 pad_maximum_fusion
  67.1 12.1 %gather_fusion = bf16[4096,67]{1,0:T(8,128)(2,1)S(1)} fusion(bf16[67,2048]{0,1:T(8,128)(2,1)S(1)} %pad_maximum_fusion, s32[4096]{0:T(1024)S(1)} %fusion.19), kind=kCustom, calls=%fused_computation | custom fusion | bytes 1114112 | tf_op jit(solution)/shard_map/jit(_take)/gather | solution.py:47
  79.2 0.6 copy.30
  79.8 0.9 select_select_fusion
  80.7 0.0 all-to-all-done.1
  80.8 9.2 %all-to-all-start = ((bf16[67,32,128]{2,0,1:T(8,128)(2,1)}), bf16[67,32,128]{2,0,1:T(8,128)(2,1)S(1)}, u32[]{:S(2)}, u32[]{:S(2)}) async-start(bf16[67,32,128]{2,0,1:T(8,128)(2,1)} %select_select_fusion), calls=%async_computation | async-start | bytes 1179648 | tf_op jit(solution)/shard_map/all_to_all | solution.py:50
  90.0 0.9 iota_compare_fusion.7
  90.9 15.6 %all-to-all-done = bf16[67,32,128]{2,0,1:T(8,128)(2,1)S(1)} async-done(((bf16[67,32,128]{2,0,1:T(8,128)(2,1)}), bf16[67,32,128]{2,0,1:T(8,128)(2,1)S(1)}, u32[]{:S(2)}, u32[]{:S(2)}) %all-to-all-start) | async-done | bytes 548896 | tf_op jit(solution)/shard_map/all_to_all | solution.py:50
  106.6 0.0 copy-done
  106.6 13.2 %fusion.9 = bf16[1536,128]{1,0:T(8,128)(2,1)S(1)} fusion(bf16[64,1536]{1,0:T(8,128)(2,1)S(1)} %copy-done, f32[4096]{0:T(1024)S(1)} %get-tuple-element.3, f32[4096]{0:T(1024)S(1)} %get-tuple-element.4, f32[4096]{0:T(1024)S(1)} %get-tuple-element.2, bf16[67,32,128]{2,0,1:T(8,128)(2,1)S(1)} %all-to-all-done, pred[4096,128]{1,0:T(32,128)(4,1)S(1)} %iota_compare_fusion.7), kind=kOutput, calls=%fused_computation.16 | convolution fusion | flops 2447769600 | bytes 1687552 | tf_op jit(solution)/shard_map/dot_general | solution.py:59
  119.8 0.0 copy-start.2
  119.8 7.3 %tile.2 = bf16[1536,32,128]{2,0,1:T(8,128)(2,1)} broadcast(bf16[1536,128]{1,0:T(8,128)(2,1)S(1)} %fusion.9), dimensions={0,2} | broadcast | bytes 12976128 | tf_op jit(solution)/shard_map/tile | solution.py:64
  127.1 279.1 %all_to_all.29 = bf16[1536,32,128]{2,0,1:T(8,128)(2,1)} all-to-all(bf16[1536,32,128]{2,0,1:T(8,128)(2,1)} %tile.2), channel_id=1, replica_groups=mesh['paths'=8,'cpty'=32] {'cpty'}, dimensions={1} | all-to-all | bytes 25165824 | tf_op jit(solution)/shard_map/all_to_all | solution.py:63
  406.2 16.6 %copy.33 = bf16[1536,32,128]{0,2,1:T(8,128)(2,1)} copy(bf16[1536,32,128]{2,0,1:T(8,128)(2,1)} %all_to_all.29) | data formatting | bytes 25165824 | tf_op jit(solution)/shard_map/all_to_all | solution.py:63
  422.8 0.0 copy-done.2
  422.8 6.5 %convolution_convert_fusion = bf16[4096,128]{1,0:T(8,128)(2,1)S(1)} fusion(bf16[1536,4096]{0,1:T(8,128)(2,1)} %bitcast.86, bf16[1536,128]{1,0:T(8,128)(2,1)S(1)} %fusion.9), kind=kOutput, calls=%fused_computation.14 | convolution fusion | flops 1611137024 | bytes 14024704 | tf_op jit(solution)/shard_map/pa,pb->ab/dot_general | solution.py:69
  429.4 22.6 %all_to_all.30 = bf16[8,512,128]{2,1,0:T(8,128)(2,1)S(1)} all-to-all(bf16[8,512,128]{2,1,0:T(8,128)(2,1)S(1)} %bitcast.88), channel_id=1, replica_groups=mesh['paths'=8,'cpty'=32] {'paths'}, dimensions={0} | all-to-all | bytes 2097152 | tf_op jit(solution)/shard_map/all_to_all | solution.py:16
  451.9 0.1 convert_reduce_fusion
  452.1 0.7 broadcast_multiply_fusion
  (9 shorter events, 0.1 us)
Async XLA Ops:
  0.6 105.9 %copy-start = (bf16[64,1536]{1,0:T(8,128)(2,1)S(1)}, bf16[64,1536]{1,0:T(8,128)(2,1)}, u32[]{:S(2)}) copy-start(bf16[64,1536]{1,0:T(8,128)(2,1)} %param.6) | copy-start | bytes 589828
  0.6 19.6 %copy-start.1 = (s32[2048]{0:T(1024)S(1)}, s32[2048]{0:T(1024)}, u32[]{:S(2)}) copy-start(s32[2048]{0:T(1024)} %param.11) | copy-start | bytes 24580
  0.7 64.4 %copy-start.3 = (bf16[64,2048]{1,0:T(8,128)(2,1)S(1)}, bf16[64,2048]{1,0:T(8,128)(2,1)}, u32[]{:S(2)}) copy-start(bf16[64,2048]{1,0:T(8,128)(2,1)} %param.7) | copy-start | bytes 786436
  0.7 64.7 %copy-start.4 = (bf16[2048]{0:T(1024)(128)(2,1)S(1)}, bf16[2048]{0:T(1024)(128)(2,1)}, u32[]{:S(2)}) copy-start(bf16[2048]{0:T(1024)(128)(2,1)} %param.8) | copy-start | bytes 12292
  0.7 65.0 %copy-start.5 = (bf16[2048]{0:T(1024)(128)(2,1)S(1)}, bf16[2048]{0:T(1024)(128)(2,1)}, u32[]{:S(2)}) copy-start(bf16[2048]{0:T(1024)(128)(2,1)} %param.9) | copy-start | bytes 12292
  0.7 65.4 %copy-start.6 = (bf16[2048]{0:T(1024)(128)(2,1)S(1)}, bf16[2048]{0:T(1024)(128)(2,1)}, u32[]{:S(2)}) copy-start(bf16[2048]{0:T(1024)(128)(2,1)} %param.10) | copy-start | bytes 12292
  53.0 27.7 %all-to-all-start.1 = ((s32[1,32,128]{2,0,1:T(1,128)}), s32[1,32,128]{2,0,1:T(1,128)S(1)}, u32[]{:S(2)}, u32[]{:S(2)}) async-start(s32[1,32,128]{2,0,1:T(1,128)} %bitcast.12), calls=%async_computation.1 | async-start | bytes 32768 | tf_op jit(solution)/shard_map/all_to_all | solution.py:51
  80.8 25.8 %all-to-all-start = ((bf16[67,32,128]{2,0,1:T(8,128)(2,1)}), bf16[67,32,128]{2,0,1:T(8,128)(2,1)S(1)}, u32[]{:S(2)}, u32[]{:S(2)}) async-start(bf16[67,32,128]{2,0,1:T(8,128)(2,1)} %select_select_fusion), calls=%async_computation | async-start | bytes 1179648 | tf_op jit(solution)/shard_map/all_to_all | solution.py:50
  119.8 303.0 %copy-start.2 = (bf16[1536,128]{1,0:T(8,128)(2,1)}, bf16[1536,128]{1,0:T(8,128)(2,1)S(1)}, u32[]{:S(2)}) copy-start(bf16[1536,128]{1,0:T(8,128)(2,1)S(1)} %fusion.9) | copy-start | bytes 1179652
